TPU v7x, 32 devices: a whole 2x2x4 slice. The times are simulated.
32 devices in a mesh: cand: 4 (over x, core), tp: 8 (over z, y).
Axes of the slice: x: 2, y: 2, z: 4, core: 2. Of those that a mesh axis runs over, the one named last changes fastest.
Arguments:
- start_state: float32 [128], replicated, may hold values from -6 to 6
- goal: float32 [128], replicated, may hold values from -6 to 6
- mean_prev: float32 [128], replicated, may hold values from -0.5 to 0.5
- std_prev: float32 [128], replicated, may hold values from 0.1 to 0.5
- noise: float32 [768, 128], P('cand'), may hold values from -23 to 23
- members: int32 [768, 1], P('cand'), may hold values from 0 to 3; in each aligned block of 192 rows (0 to 191, 192 to 383, ...) at most 60 rows name the same one
- elites: int32 [96], replicated, may hold values from 0 to 767, as said below
- w_in: bfloat16 [4, 144, 4096], P(None, None, 'tp'), may hold values from -0.5 to 0.5
- w_hid: bfloat16 [4, 4096, 4096], P(None, None, 'tp'), may hold values from -0.09375 to 0.09375
- w_out: bfloat16 [4, 4096, 128], P(None, 'tp'), may hold values from -0.09375 to 0.09375
Outputs:
- scores: float32 [768], P('cand')
- new_mean: float32 [128], replicated
- new_std: float32 [128], replicated
Inputs may be any that keep to these rules, and one draw needn't show every extreme that they name: `members`: among the candidates of one index of cand no member is named more than 60 times. `elites`: 96 distinct candidate numbers.
All inputs are finite; a program needn't handle non-finite values.
Results may differ from a plain program's by a relative error of at most 0.0085.
Values may be sent and summed in bfloat16 or wider, within the bound.
A program may use at most 64 MiB of HBM per device.

v0:
```python
import functools
import jax
import jax.numpy as jnp
from jax import lax
from jax.experimental import pallas as pl
from jax.experimental.pallas import tpu as pltpu
from jax.sharding import PartitionSpec as P

HORIZON = 8
F32 = jnp.float32
BF16 = jnp.bfloat16
HI = lax.Precision.HIGHEST


def silu(v):
    h = 0.5 * v
    return h + h * jnp.tanh(h)


def kernel(
    n_cand, n_tp, cap,
    start_ref, goal_ref, mean_ref, std_ref, noise_ref, members_ref, elites_ref,
    win_hbm, whid_hbm, wout_hbm,
    scores_ref, new_mean_ref, new_std_ref,
    win_v, whid_v, wout_v, h1_v, pf, ps, rs_rx, xs, xs_send, state, sq, big,
    act_send, act_rx, act_t, sa_all, meta_all, ret_all,
    load_sem, win_s, win_r, act_s, act_r, sa_s, sa_r, meta_s, meta_r,
    rs_s, rs_r, ag_s, ag_r, ret_s, ret_r,
):
    n_mem = win_hbm.shape[0]
    chunk = win_hbm.shape[2]
    width = start_ref.shape[1]
    local = noise_ref.shape[0]
    rows = n_mem * cap
    lowest = n_tp // 4
    owners = range(lowest, n_tp - lowest)
    n_own = len(owners)
    own = rows // n_own
    a_dim = mean_ref.shape[1] // HORIZON
    c = lax.axis_index("cand")
    t = lax.axis_index("tp")
    m = lax.rem(c, n_mem)
    group = c - m

    def tp_peer(d):
        return lax.rem(t + d, n_tp)

    def remote(src, dst, s, r, cc, tt):
        return pltpu.make_async_remote_copy(
            src_ref=src, dst_ref=dst, send_sem=s, recv_sem=r,
            device_id={"cand": cc, "tp": tt}, device_id_type=pl.DeviceIdType.MESH,
        )

    pair = t + 1 - 2 * lax.rem(t, 2)
    win_copies = [
        remote(win_hbm.at[m], win_v.at[t], win_s.at[d], win_r.at[t], c, pair if d == 1 else tp_peer(d))
        for d in [1] + list(range(2, n_tp, 2))
    ]
    for cp in win_copies:
        cp.start()

    def arrived(d):
        src = lax.rem(t + n_tp - d, n_tp)
        return remote(win_hbm.at[m], win_v.at[src], win_s.at[0], win_r.at[src], c, pair)

    loads = [
        pltpu.make_async_copy(win_hbm.at[m], win_v.at[t], load_sem.at[0]),
        pltpu.make_async_copy(whid_hbm.at[m], whid_v, load_sem.at[1]),
    ]
    loads.append(pltpu.make_async_copy(wout_hbm.at[m], wout_v, load_sem.at[2]))
    for cp in loads:
        cp.start()

    actions = mean_ref[...] + std_ref[...] * noise_ref[...]
    members = members_ref[...]
    lane = lax.broadcasted_iota(jnp.int32, (local, 128), 1)
    onehot = (members == lane).astype(F32)
    lower = (
        lax.broadcasted_iota(jnp.int32, (local, local), 1)
        < lax.broadcasted_iota(jnp.int32, (local, local), 0)
    ).astype(BF16)
    before = jnp.dot(lower, onehot.astype(BF16), preferred_element_type=F32)
    position = jnp.sum(before * onehot, axis=1, keepdims=True).astype(jnp.int32)
    slot = members * cap + position
    place = slot == lax.broadcasted_iota(jnp.int32, (local, rows), 1)
    place_f = place.astype(F32)
    over_cands = (((0,), (0,)), ((), ()))
    act_send[...] = lax.dot_general(
        place_f.astype(BF16), actions.astype(BF16), over_cands, preferred_element_type=F32
    ).astype(BF16)
    mine = pl.multiple_of(m * cap, cap)
    act_copies = []
    for k in range(1, n_mem):
        m2 = lax.rem(m + k, n_mem)
        act_copies.append(remote(
            act_send.at[pl.ds(pl.multiple_of(m2 * cap, cap), cap), :],
            act_rx.at[pl.ds(mine, cap), :], act_s.at[k], act_r.at[k], group + m2, t))
    for cp in act_copies:
        cp.start()
    act_rx[pl.ds(mine, cap), :] = act_send[pl.ds(mine, cap), :]

    numbers = c * local + lax.broadcasted_iota(jnp.int32, (local, 1), 0)
    chosen = jnp.sum((numbers == elites_ref[...]).astype(F32), axis=1, keepdims=True)
    action_cost = jnp.sum(actions * actions, axis=1, keepdims=True) * (0.1 / a_dim)
    facts = jnp.where(lane == 0, 1.0, jnp.where(lane == 1, chosen, jnp.where(lane == 2, action_cost, 0.0)))
    sa_all[c] = lax.dot_general(place_f, actions, over_cands, precision=HI, preferred_element_type=F32)
    meta_all[c] = lax.dot_general(facts, place_f, over_cands, precision=HI, preferred_element_type=F32)[:8]
    side_copies = []
    for k in range(1, n_cand):
        c2 = lax.rem(c + k, n_cand)
        side_copies.append(remote(meta_all.at[c], meta_all.at[c], meta_s.at[k], meta_r.at[k], c2, t))
        side_copies.append(remote(sa_all.at[c], sa_all.at[c], sa_s.at[k], sa_r.at[k], c2, t))
    for cp in side_copies:
        cp.start()

    state[...] = jnp.broadcast_to(start_ref[...], state.shape)
    sq[...] = jnp.zeros_like(sq)
    xs[...] = jnp.broadcast_to(start_ref[...], xs.shape).astype(BF16)
    for cp in act_copies:
        cp.wait_recv()
    for s in range(HORIZON):
        act_t[s] = act_rx[...].astype(F32)[:, s * a_dim:(s + 1) * a_dim].astype(BF16)
    for cp in loads:
        cp.wait()
    for d in range(2, n_tp, 2):
        arrived(d).wait_recv()
        src = lax.rem(t + n_tp - d, n_tp)
        cp = remote(win_v.at[src], win_v.at[src], win_s.at[d + 1], win_r.at[src], c, pair)
        cp.start()
        win_copies.append(cp)
    for d in range(1, n_tp, 2):
        arrived(d).wait_recv()

    half = min(256, chunk)
    owner = jnp.logical_and(t >= owners[0], t <= owners[-1])
    place_own = t - lowest
    first_own = pl.multiple_of(place_own * own, own)

    def step_body(step, carry):
        rs = [
            remote(ps.at[pl.ds(i * own, own), :], rs_rx.at[t], rs_s.at[i], rs_r.at[t], c, o)
            for i, o in enumerate(owners)
        ]
        for q in range(2):
            lo, hi = q * rows // 2, (q + 1) * rows // 2
            held = range(q * n_own // 2, (q + 1) * n_own // 2)

            @pl.when(step > 0)
            def _():
                for i in held:
                    pl.when(t != owners[i])(remote(
                        xs_send, xs.at[pl.ds(i * own, own), :], ag_s.at[0], ag_r.at[i], c, pair).wait_recv)

            x = jnp.concatenate([xs[lo:hi, :], act_t[step, lo:hi, :]], axis=1)
            for d in range(n_tp):
                h1_v[lo:hi, d * chunk:(d + 1) * chunk] = silu(
                    jnp.dot(x, win_v[d], preferred_element_type=F32)).astype(BF16)
            total = None
            for n in range(chunk // half):
                h2 = silu(jnp.dot(h1_v[lo:hi, :], whid_v[:, n * half:(n + 1) * half],
                                  preferred_element_type=F32)).astype(BF16)
                part = jnp.dot(h2, wout_v[n * half:(n + 1) * half, :], preferred_element_type=F32)
                total = part if total is None else total + part
            pf[lo:hi, :] = total
            ps[lo:hi, :] = total.astype(BF16)
            for i in held:
                pl.when(t != owners[i])(rs[i].start)

        @pl.when(owner)
        def _():
            change = pf[pl.ds(first_own, own), :]
            for d in range(1, n_tp):
                src = lax.rem(t + n_tp - d, n_tp)
                remote(ps.at[pl.ds(0, own), :], rs_rx.at[src], rs_s.at[0], rs_r.at[src], c, pair).wait_recv()
                change = change + rs_rx[src].astype(F32)
            new_state = state[...] + change
            state[...] = new_state

            ag = [
                remote(xs_send, xs.at[pl.ds(first_own, own), :], ag_s.at[d], ag_r.at[place_own], c, tp_peer(d))
                for d in range(1, n_tp)
            ]

            @pl.when(step < HORIZON - 1)
            def _():
                xs_send[...] = new_state.astype(BF16)
                for cp in ag:
                    cp.start()
                xs[pl.ds(first_own, own), :] = new_state.astype(BF16)

            gap = new_state - goal_ref[...]
            sq[...] += gap * gap

            @pl.when(step < HORIZON - 1)
            def _():
                for cp in ag:
                    cp.wait_send()

        for o, cp in zip(owners, rs):
            pl.when(t != o)(cp.wait_send)

        return carry

    lax.fori_loop(0, HORIZON, step_body, 0)

    me = c * n_own + place_own
    ret_copies = [
        remote(ret_all.at[me], ret_all.at[me], ret_s.at[kc * n_tp + kt], ret_r.at[me],
               lax.rem(c + kc, n_cand), tp_peer(kt))
        for kc in range(n_cand) for kt in range(n_tp) if kc + kt
    ]

    @pl.when(owner)
    def _():
        big[...] = jnp.zeros_like(big)
        big[pl.ds(pl.multiple_of(m * cap + lax.rem(first_own, cap), own), own), :] = sq[...] * (1.0 / width)
        row = lax.dot_general(jnp.ones((8, width), F32), big[...], (((1,), (1,)), ((), ())),
                              precision=HI, preferred_element_type=F32)
        ret_all[me] = row[0:1]
        for cp in ret_copies:
            cp.start()

    for cp in side_copies:
        cp.wait_recv()
    for cc in range(n_cand):
        for i, o in enumerate(owners):
            k = cc * n_own + i
            pl.when(jnp.logical_or(t != o, c != cc))(remote(
                ret_all.at[k], ret_all.at[k], ret_s.at[0], ret_r.at[k], c, pair).wait_recv)

    per_block = cap // own
    returns = []
    for b in range(n_cand):
        parts = [ret_all[(b - b % n_mem + m2) * n_own + b % n_mem * per_block + h]
                 for m2 in range(n_mem) for h in range(per_block)]
        returns.append(-functools.reduce(jnp.add, parts) - meta_all[b, 2:3, :])
    count = local * n_cand

    def over(vals):
        return jnp.sum(functools.reduce(jnp.add, vals), axis=1, keepdims=True)

    valid = [meta_all[b, 0:1, :] for b in range(n_cand)]
    mean = over([valid[b] * returns[b] for b in range(n_cand)]) / count
    var = over([valid[b] * (returns[b] - mean) ** 2 for b in range(n_cand)]) / count
    scale = jnp.sqrt(var + 1e-06)
    scores = [(returns[b] - mean) / scale for b in range(n_cand)]
    weights = [meta_all[b, 1:2, :] * (0.5 + 1.0 / (1.0 + jnp.exp(-scores[b]))) for b in range(n_cand)]
    weight_sum = over(weights)

    def moment(values):
        rows8 = [jnp.broadcast_to(weights[b], (8, rows)) for b in range(n_cand)]
        return functools.reduce(jnp.add, [
            jnp.dot(rows8[b], values(b), precision=HI, preferred_element_type=F32)
            for b in range(n_cand)])[0:1] / weight_sum

    new_mean = moment(lambda b: sa_all[b])
    new_mean_ref[...] = new_mean
    new_std_ref[...] = jnp.sqrt(moment(lambda b: (sa_all[b] - new_mean) ** 2) + 1e-06)

    my_parts = [ret_all[(group + m2) * n_own + m * per_block + h]
                for m2 in range(n_mem) for h in range(per_block)]
    my_returns = -functools.reduce(jnp.add, my_parts) - meta_all[c, 2:3, :]
    my_scores = jnp.broadcast_to((my_returns - mean) / scale, (8, rows))
    scores_ref[...] = lax.dot_general(my_scores, place_f, (((1,), (1,)), ((), ())),
                                      precision=HI, preferred_element_type=F32)[0:1]

    for cp in win_copies + act_copies + side_copies:
        cp.wait_send()

    @pl.when(owner)
    def _():
        for cp in ret_copies:
            cp.wait_send()


def on_device(n_cand, n_tp, start_state, goal, mean_prev, std_prev, noise, members, elites, w_in, w_hid, w_out):
    local = noise.shape[0]
    n_mem, depth, chunk = w_in.shape
    width = start_state.shape[0]
    flat = mean_prev.shape[0]
    hidden = w_hid.shape[1]
    cap = -(-(5 * local // 16) // 16) * 16
    rows = n_mem * cap
    n_own = n_tp - 2 * (n_tp // 4)
    own = rows // n_own
    total = n_cand * n_tp
    vmem = pl.BlockSpec(memory_space=pltpu.VMEM)
    hbm = pl.BlockSpec(memory_space=pl.ANY)
    dma = pltpu.SemaphoreType.DMA
    scores, new_mean, new_std = pl.pallas_call(
        functools.partial(kernel, n_cand, n_tp, cap),
        out_shape=(
            jax.ShapeDtypeStruct((1, local), F32),
            jax.ShapeDtypeStruct((1, flat), F32),
            jax.ShapeDtypeStruct((1, flat), F32),
        ),
        in_specs=[vmem] * 7 + [hbm] * 3,
        out_specs=(vmem,) * 3,
        scratch_shapes=[
            pltpu.VMEM((n_tp, depth, chunk), BF16),
            pltpu.VMEM((hidden, chunk), BF16),
            pltpu.VMEM((chunk, width), BF16),
            pltpu.VMEM((rows, hidden), BF16),
            pltpu.VMEM((rows, width), F32),
            pltpu.VMEM((rows, width), BF16),
            pltpu.VMEM((n_tp, own, width), BF16),
            pltpu.VMEM((rows, width), BF16),
            pltpu.VMEM((own, width), BF16),
            pltpu.VMEM((own, width), F32),
            pltpu.VMEM((own, width), F32),
            pltpu.VMEM((rows, width), F32),
            pltpu.VMEM((rows, flat), BF16),
            pltpu.VMEM((rows, flat), BF16),
            pltpu.VMEM((HORIZON, rows, flat // HORIZON), BF16),
            pltpu.VMEM((n_cand, rows, flat), F32),
            pltpu.VMEM((n_cand, 8, rows), F32),
            pltpu.VMEM((n_cand * n_own, 1, rows), F32),
            dma((3,)),
            dma((n_tp,)), dma((n_tp,)),
            dma((n_mem,)), dma((n_mem,)),
            dma((n_cand,)), dma((n_cand,)),
            dma((n_cand,)), dma((n_cand,)),
            dma((n_tp,)), dma((n_tp,)),
            dma((n_tp,)), dma((n_tp,)),
            dma((total,)), dma((total,)),
        ],
        compiler_params=pltpu.CompilerParams(has_side_effects=True, vmem_limit_bytes=56 << 20),
    )(
        start_state.reshape(1, -1), goal.reshape(1, -1), mean_prev.reshape(1, -1),
        std_prev.reshape(1, -1), noise, members, elites.reshape(1, -1), w_in, w_hid, w_out,
    )
    return scores.reshape(-1), new_mean.reshape(-1), new_std.reshape(-1)


def solution(mesh):
    placed = (
        P(), P(), P(), P(), P("cand", None), P("cand", None), P(),
        P(None, None, "tp"), P(None, None, "tp"), P(None, "tp", None),
    )
    return jax.shard_map(
        functools.partial(on_device, mesh.shape["cand"], mesh.shape["tp"]),
        mesh=mesh, in_specs=placed, out_specs=(P("cand"), P(), P()), check_vma=False,
    )
```

profile of v0, /device:TPU:0, one launch (start us, length us, event | category | flops | bytes accessed | tf_op | source)
XLA Modules:
  0.0 115.9 jit_solution(10298567908774377290)
XLA Ops:
  0.6 1.4 %copy.13.members_ref = s32[192,1]{1,0:T(8,128)} copy(s32[192,1]{0,1:T(1,128)} %param.15) | data formatting | bytes 1536 | tf_op args[5]
  2.1 110.3 %shard_map.121 = (f32[1,192]{1,0:T(1,128)}, f32[1,128]{1,0:T(1,128)}, f32[1,128]{1,0:T(1,128)}) custom-call(f32[1,128]{1,0:T(1,128)} %bitcast.9, f32[1,128]{1,0:T(1,128)} %bitcast.10, f32[1,128]{1,0:T(1,128)} %bitcast.11, f32[1,128]{1,0:T(1,128)} %bitcast.12, f32[192,128]{1,0:T(8,128)} %noise_ref.1, s32[192,1]{1,0:T(8,128)} %copy.13.members_ref, ...), custom_call_target="tpu_custom_call" | custom-call | tf_op jit(solution)/shard_map/pallas_call | solution.py:290
  112.4 1.2 %copy.17 = f32[192]{0:T(256)} copy(f32[192]{0:T(256)} %bitcast.8) | data formatting | bytes 1536
  113.6 1.1 copy.18
  114.7 1.2 %copy.19 = f32[128]{0:T(128)} copy(f32[128]{0:T(128)} %bitcast.14) | data formatting | bytes 1024
where the time goes:
time: 116 us
  Pallas kernels  110 us (95%)
  local copies, waits for them, and re-layouts  4.96 us (4%)
    pallas_call x1, Pallas kernels, on_device(): pl.pallas_call(functools.partial(kernel, n_cand, n_tp, cap), out_shape=(j...  110 us
    unnamed x4, local copies, waits for them, and re-layouts  4.96 us

commit v1 on v0

v1 whole, which is shorter than its diff:
```python
import functools
import jax
import jax.numpy as jnp
from jax import lax
from jax.experimental import pallas as pl
from jax.experimental.pallas import tpu as pltpu
from jax.sharding import PartitionSpec as P

HORIZON = 8
BATCH = 128
F32 = jnp.float32
BF16 = jnp.bfloat16
HI = lax.Precision.HIGHEST


def silu_of_half(h):
    return h + h * jnp.tanh(h)


def kernel(
    n_cand, n_tp, cap,
    start_ref, goal_ref, mean_ref, std_ref, noise_ref, members_ref, elites_ref,
    win_hbm, whid_hbm, wout_hbm,
    out_ref,
    win_v, bias_v, whid_v, wout_v, h1_v, pf, rs_rx, xs, xs_send, state, sq, big,
    act_send, act_rx, sa_all, meta_all, ret_all,
    win_sem, whid_sem, wout_sem, wa_s, wa_r, bias_s, bias_r, ws_s, ws_r,
    act_s, act_r, sa_s, sa_r, meta_s, meta_r,
    rs_s, rs_r, ag_s, ag_r, ret_s, ret_r,
):
    n_mem = win_hbm.shape[0]
    depth = win_hbm.shape[1]
    chunk = win_hbm.shape[2]
    width = start_ref.shape[1]
    flat = mean_ref.shape[1]
    local = noise_ref.shape[0]
    rows = n_mem * cap
    batches = rows // BATCH
    n_work = 2 * batches
    per_batch = BATCH // cap
    lowest = n_tp // 4
    owners = range(lowest, n_tp - lowest)
    n_own = len(owners)
    own = BATCH // n_own
    a_dim = flat // HORIZON
    c = lax.axis_index("cand")
    t = lax.axis_index("tp")
    m = lax.rem(c, n_mem)
    group = c - m
    side = lax.rem(c, 2)
    first = m - side
    worker = side == 1
    owner = jnp.logical_and(t >= owners[0], t <= owners[-1])
    place_own = t - lowest
    first_own = pl.multiple_of(place_own * own, own)
    upper = t >= n_tp // 2

    def tp_peer(d):
        return lax.rem(t + d, n_tp)

    def tp_from(d):
        return lax.rem(t + n_tp - d, n_tp)

    def outer_first(i, n):
        return jnp.where(upper, i, n - 1 - i)

    def remote(src, dst, s, r, cc, tt):
        return pltpu.make_async_remote_copy(
            src_ref=src, dst_ref=dst, send_sem=s, recv_sem=r,
            device_id={"cand": cc, "tp": tt}, device_id_type=pl.DeviceIdType.MESH,
        )

    def wa_copy(mi, src, d, tt):
        return remote(
            win_hbm.at[first + mi, pl.ds(width, a_dim), :], win_v.at[mi, src, pl.ds(width, a_dim), :],
            wa_s.at[mi, d], wa_r.at[mi, src], c, tt)

    def bias_copy(mi, src, d, tt):
        return remote(bias_v.at[mi, src], bias_v.at[mi, src], bias_s.at[mi, d], bias_r.at[mi, src], c, tt)

    n_z = 4
    n_y = n_tp // n_z
    z, y = t // n_y, lax.rem(t, n_y)
    rows_s = pl.ds(0, width)

    def ws_copy(mi, src_z, e, own_slice, cc, tt):
        src = src_z * n_y + y
        held = win_hbm.at[first + mi, rows_s, :] if own_slice else win_v.at[mi, src, rows_s, :]
        return remote(held, win_v.at[mi, src, rows_s, :], ws_s.at[mi, src_z, e], ws_r.at[mi, src], cc, tt)

    def ws_own(mi, act):
        pl.when(z < n_z - 1)(act(ws_copy(mi, z, n_y, True, c, t + n_y)))
        pl.when(z > 0)(act(ws_copy(mi, z, n_y + 1, True, c, t - n_y)))
        for e in range(n_y):
            pl.when(y != e)(act(ws_copy(mi, z, e, True, c + 1, z * n_y + e)))

    def ws_relayed(mi, hop, up, act):
        src_z = z - hop if up else z + hop
        there = src_z >= 0 if up else src_z < n_z
        onward = z < n_z - 1 if up else z > 0
        beyond = ws_copy(mi, src_z, n_y if up else n_y + 1, False, c, t + n_y if up else t - n_y)
        pl.when(jnp.logical_and(there, onward))(act(beyond))
        for e in range(n_y):
            pl.when(there)(act(ws_copy(mi, src_z, e, False, c + 1, z * n_y + e)))

    def ws_arrived(mi, src):
        return remote(
            win_hbm.at[first + mi, rows_s, :], win_v.at[mi, src, rows_s, :], ws_s.at[mi, 0, 0], ws_r.at[mi, src], c, t)

    def ws_serve():
        for mi in range(2):
            ws_own(mi, lambda cp: cp.start)
        for hop in range(1, n_z):
            for mi in range(2):
                for up in (True, False):
                    src_z = z - hop if up else z + hop
                    there = src_z >= 0 if up else src_z < n_z
                    pl.when(there)(ws_arrived(mi, src_z * n_y + y).wait_recv)
                    ws_relayed(mi, hop, up, lambda cp: cp.start)

    def ws_served():
        for mi in range(2):
            ws_own(mi, lambda cp: cp.wait_send)
            for hop in range(1, n_z):
                for up in (True, False):
                    ws_relayed(mi, hop, up, lambda cp: cp.wait_send)

    def win_load(mi):
        return pltpu.make_async_copy(
            win_hbm.at[first + mi], win_v.at[mi, t, pl.ds(0, depth), :], win_sem.at[mi])

    def whid_load(mi):
        return pltpu.make_async_copy(whid_hbm.at[first + mi], whid_v.at[mi], whid_sem.at[mi])

    def wout_load(mi):
        return pltpu.make_async_copy(wout_hbm.at[first + mi], wout_v.at[mi], wout_sem.at[mi])

    @pl.when(worker)
    def _():
        for mi in range(2):
            win_load(mi).start()
        for mi in range(2):
            for d in range(1, n_tp):
                wa_copy(mi, t, d, tp_peer(d)).start()
        for mi in range(2):
            whid_load(mi).start()
            wout_load(mi).start()

    actions = mean_ref[...] + std_ref[...] * noise_ref[...]
    members = members_ref[...]
    onehot = (members == lax.broadcasted_iota(jnp.int32, (16, local), 0)).astype(F32)
    lower = (
        lax.broadcasted_iota(jnp.int32, (local, local), 0)
        < lax.broadcasted_iota(jnp.int32, (local, local), 1)
    ).astype(BF16)
    before = jnp.dot(onehot.astype(BF16), lower, preferred_element_type=F32)
    position = jnp.sum(before * onehot, axis=0, keepdims=True).astype(jnp.int32)
    slot = members * cap + position
    place_f = (slot == lax.broadcasted_iota(jnp.int32, (rows, local), 0)).astype(F32)
    act_send[...] = jnp.dot(
        place_f.astype(BF16), actions.astype(BF16), preferred_element_type=F32).astype(BF16)

    def act_copy(i):
        return remote(
            act_send.at[pl.ds(2 * i * cap, 2 * cap), :], act_rx.at[m], act_s.at[i], act_r.at[m],
            group + 2 * i + 1, t)

    for i in range(n_mem // 2):
        pl.when(c != group + 2 * i + 1)(act_copy(i).start)

    @pl.when(worker)
    def _():
        act_rx[m] = act_send[pl.ds(pl.multiple_of(first * cap, cap), 2 * cap), :]
        half_start = (0.5 * jnp.broadcast_to(start_ref[...], (16, width))).astype(BF16)
        for mi in range(2):
            win_load(mi).wait()
            bias_v[mi, t] = jnp.dot(
                half_start, win_v[mi, t, 0:width, :], preferred_element_type=F32)[0:1]
            for d in range(1, n_tp):
                bias_copy(mi, t, d, tp_peer(d)).start()

    lane = lax.broadcasted_iota(jnp.int32, (local, 128), 1)
    numbers = c * local + lax.broadcasted_iota(jnp.int32, (local, 1), 0)
    chosen = jnp.sum((numbers == elites_ref[...]).astype(F32), axis=1, keepdims=True)
    action_cost = jnp.sum(actions * actions, axis=1, keepdims=True) * (0.1 / a_dim)
    facts = jnp.where(lane == 0, 1.0, jnp.where(lane == 1, chosen, jnp.where(lane == 2, action_cost, 0.0)))
    sa_all[c] = jnp.dot(place_f, actions, precision=HI, preferred_element_type=F32)
    meta_all[c] = lax.dot_general(facts, place_f, (((0,), (1,)), ((), ())), precision=HI, preferred_element_type=F32)[:8]
    side_copies = []
    for k in range(1, n_cand):
        c2 = lax.rem(c + k, n_cand)
        side_copies.append(remote(meta_all.at[c], meta_all.at[c], meta_s.at[k], meta_r.at[k], c2, t))
        side_copies.append(remote(sa_all.at[c], sa_all.at[c], sa_s.at[k], sa_r.at[k], c2, t))
    for cp in side_copies:
        cp.start()

    pl.when(jnp.logical_not(worker))(ws_serve)

    half = min(256, chunk)

    def rs_copy(k, i, src):
        return remote(
            pf.at[k, pl.ds(pl.multiple_of(i * own, own), own), :], rs_rx.at[k, src], rs_s.at[k, i], rs_r.at[k, src],
            c, lowest + i)

    def ag_copy(k, i, dst):
        return remote(
            xs_send.at[k], xs.at[k, pl.ds(pl.multiple_of(i * own, own), own), :], ag_s.at[k, dst], ag_r.at[k, i],
            c, dst)

    lanes = lax.broadcasted_iota(jnp.int32, (1, flat), 1)

    def masked_actions(step, mi, q):
        lo = step * a_dim
        keep = jnp.where(jnp.logical_and(lanes >= lo, lanes < lo + a_dim), 0.5, 0.0).astype(BF16)
        rows_of = pl.ds(pl.multiple_of(mi * cap, cap), cap)
        acts = jnp.concatenate([act_rx[q * per_batch + b, rows_of, :] for b in range(per_batch)], axis=0)
        return acts * keep

    def contribute(k, mi):
        total = None
        for n in range(chunk // half):
            h2 = silu_of_half(0.5 * jnp.dot(
                h1_v[...], whid_v[mi, :, n * half:(n + 1) * half], preferred_element_type=F32)).astype(BF16)
            part = jnp.dot(h2, wout_v[mi, n * half:(n + 1) * half, :], preferred_element_type=F32)
            total = part if total is None else total + part
        pf[k] = total
        for i in range(n_own):
            o = outer_first(i, n_own)
            pl.when(t != lowest + o)(rs_copy(k, o, t).start)

    def reduce(k):
        change = pf[k, pl.ds(first_own, own), :]
        for d in range(1, n_tp):
            src = tp_from(d)
            rs_copy(k, 0, src).wait_recv()
            change = change + rs_rx[k, src]
        new_state = state[k] + change
        state[k] = new_state
        gap = new_state - goal_ref[...]
        sq[k] += gap * gap
        return new_state

    def broadcast(k, new_state):
        half_state = (0.5 * new_state).astype(BF16)
        xs_send[k] = half_state
        for i in range(n_tp):
            dst = outer_first(i, n_tp)
            pl.when(t != dst)(ag_copy(k, place_own, dst).start)
        xs[k, pl.ds(first_own, own), :] = half_state

    def sent_rs(k):
        for i in range(n_own):
            pl.when(t != owners[i])(rs_copy(k, i, t).wait_send)

    def sent_ag(k):
        for dst in range(n_tp):
            pl.when(t != dst)(ag_copy(k, place_own, dst).wait_send)

    @pl.when(worker)
    def _():
        state[...] = jnp.broadcast_to(start_ref[...].reshape(1, 1, width), state.shape)
        sq[...] = jnp.zeros_like(sq)
        for j in range(n_mem):
            pl.when(m != j)(remote(
                act_send.at[pl.ds(0, 2 * cap), :], act_rx.at[j], act_s.at[0], act_r.at[j], c, t).wait_recv)

        def start_work(k, mi, q):
            @pl.when(q == 0)
            def _():
                for d in range(1, n_tp):
                    src = tp_from(d)
                    wa_copy(mi, src, d, t).wait_recv()
                    bias_copy(mi, src, d, t).wait_recv()
                for d in range(n_tp):
                    tile = win_v[mi, d, width:width + a_dim, :]
                    for s in range(1, HORIZON):
                        win_v[mi, d, width + s * a_dim:width + (s + 1) * a_dim, :] = tile
                whid_load(mi).wait()
                wout_load(mi).wait()

            x = masked_actions(0, mi, q)
            for d in range(n_tp):
                h1_v[:, d * chunk:(d + 1) * chunk] = silu_of_half(
                    jnp.dot(x, win_v[mi, d, width:width + flat, :], preferred_element_type=F32)
                    + bias_v[mi, d]).astype(BF16)
            contribute(k, mi)

        def next_work(step, k, mi, q):
            @pl.when(jnp.logical_and(step == 1, q == 0))
            def _():
                for d in range(1, n_tp):
                    ws_arrived(mi, tp_from(d)).wait_recv()

            for i in range(n_own):
                pl.when(t != owners[i])(ag_copy(k, i, t).wait_recv)
            sent_rs(k)
            x = jnp.concatenate([xs[k], masked_actions(step, mi, q)], axis=1)
            for d in range(n_tp):
                h1_v[:, d * chunk:(d + 1) * chunk] = silu_of_half(
                    jnp.dot(x, win_v[mi, d], preferred_element_type=F32)).astype(BF16)
            contribute(k, mi)

        def owned(step, k):
            new_state = reduce(k)

            @pl.when(step < HORIZON - 1)
            def _():
                pl.when(step > 0)(lambda: sent_ag(k))
                broadcast(k, new_state)

        def step_body(step, carry):
            def work(k, carry):
                mi = k // batches
                q = lax.rem(k, batches)
                pl.when(step == 0)(lambda: start_work(k, mi, q))
                pl.when(step > 0)(lambda: next_work(step, k, mi, q))

                def turn(e, carry):
                    late = e == 0
                    at = jnp.where(late, step - 1, step)
                    pl.when(at >= 0)(lambda: owned(at, lax.rem(e + n_work - 1, n_work)))
                    return carry

                @pl.when(owner)
                def _():
                    lax.fori_loop(k * (k - 1) // 2, jnp.minimum(k * (k + 1) // 2, n_work), turn, 0)

                return carry

            lax.fori_loop(0, n_work, work, 0)
            return carry

        lax.fori_loop(0, HORIZON, step_body, 0)
        pl.when(owner)(lambda: owned(HORIZON - 1, n_work - 1))

    chip = c // 2
    me = (chip * n_own + place_own) * batches

    def ret_copy(src, kc, kt):
        held = ret_all.at[pl.ds(src, batches)]
        return remote(held, held, ret_s.at[kc * n_tp + kt], ret_r.at[src // batches],
                      lax.rem(c + kc, n_cand), tp_peer(kt))

    far = [(kc, kt) for kc in range(n_cand) for kt in range(n_tp) if kc + kt]
    sending = jnp.logical_and(worker, owner)

    @pl.when(sending)
    def _():
        big[...] = jnp.zeros_like(big)
        for k in range(n_work):
            at = pl.multiple_of((first + k // batches) * cap + lax.rem(first_own, cap), own)
            big[k % batches, pl.ds(at, own), :] = sq[k] * (1.0 / width)
        for q in range(batches):
            row = lax.dot_general(jnp.ones((8, width), F32), big[q], (((1,), (1,)), ((), ())),
                                  precision=HI, preferred_element_type=F32)
            ret_all[me + q] = row[0:1]
        for kc, kt in far:
            ret_copy(me, kc, kt).start()

    for cp in side_copies:
        cp.wait_recv()
    for k in range(n_cand // 2 * n_own):
        o = owners[k % n_own]
        pl.when(jnp.logical_or(t != o, c != k // n_own * 2 + 1))(ret_copy(k * batches, 0, 0).wait_recv)

    split = n_own // per_batch

    def returns_of(base, j, q, h):
        parts = [ret_all[((base // 2 + p) * n_own + h * split + i) * batches + q]
                 for p in range(n_mem // 2) for i in range(split)]
        return -functools.reduce(jnp.add, parts)

    returns = []
    for b in range(n_cand):
        j = b % n_mem
        returns.append(returns_of(b - j, j, j // per_batch, j % per_batch) - meta_all[b, 2:3, :])
    count = local * n_cand

    def over(vals):
        return jnp.sum(functools.reduce(jnp.add, vals), axis=1, keepdims=True)

    valid = [meta_all[b, 0:1, :] for b in range(n_cand)]
    mean = over([valid[b] * returns[b] for b in range(n_cand)]) / count
    var = over([valid[b] * (returns[b] - mean) ** 2 for b in range(n_cand)]) / count
    scale = jnp.sqrt(var + 1e-06)
    scores = [(returns[b] - mean) / scale for b in range(n_cand)]
    weights = [meta_all[b, 1:2, :] * (0.5 + 1.0 / (1.0 + jnp.exp(-scores[b]))) for b in range(n_cand)]
    weight_sum = over(weights)

    def moment(values):
        rows8 = [jnp.broadcast_to(weights[b], (8, rows)) for b in range(n_cand)]
        return functools.reduce(jnp.add, [
            jnp.dot(rows8[b], values(b), precision=HI, preferred_element_type=F32)
            for b in range(n_cand)])[0:1] / weight_sum

    new_mean = moment(lambda b: sa_all[b])
    out_ref[1:2, 0:flat] = new_mean
    out_ref[2:3, 0:flat] = jnp.sqrt(moment(lambda b: (sa_all[b] - new_mean) ** 2) + 1e-06)

    my_returns = returns_of(group, m, m // per_batch, lax.rem(m, per_batch)) - meta_all[c, 2:3, :]
    my_scores = jnp.broadcast_to((my_returns - mean) / scale, (8, rows))
    out_ref[0:1, 0:local] = jnp.dot(my_scores, place_f, precision=HI, preferred_element_type=F32)[0:1]

    for cp in side_copies:
        cp.wait_send()
    for i in range(n_mem // 2):
        pl.when(c != group + 2 * i + 1)(act_copy(i).wait_send)

    @pl.when(worker)
    def _():
        for mi in range(2):
            for d in range(1, n_tp):
                wa_copy(mi, t, d, tp_peer(d)).wait_send()
                bias_copy(mi, t, d, tp_peer(d)).wait_send()
        for k in range(n_work):
            sent_rs(k)

    pl.when(jnp.logical_not(worker))(ws_served)

    @pl.when(sending)
    def _():
        for k in range(n_work):
            sent_ag(k)
        for kc, kt in far:
            ret_copy(me, kc, kt).wait_send()


def unpack(packed_ref, scores_ref, new_mean_ref, new_std_ref):
    for row, ref in enumerate((scores_ref, new_mean_ref, new_std_ref)):
        ref[...] = packed_ref[row:row + 1, 0:ref.shape[1]]


def on_device(n_cand, n_tp, start_state, goal, mean_prev, std_prev, noise, members, elites, w_in, w_hid, w_out):
    local = noise.shape[0]
    n_mem, depth, chunk = w_in.shape
    width = start_state.shape[0]
    flat = mean_prev.shape[0]
    hidden = w_hid.shape[1]
    cap = -(-(5 * local // 16) // 16) * 16
    rows = n_mem * cap
    batches = rows // BATCH
    n_work = 2 * batches
    n_own = n_tp - 2 * (n_tp // 4)
    own = BATCH // n_own
    total = n_cand * n_tp
    returned = n_cand // 2 * n_own
    vmem = pl.BlockSpec(memory_space=pltpu.VMEM)
    hbm = pl.BlockSpec(memory_space=pl.ANY)
    dma = pltpu.SemaphoreType.DMA
    packed = pl.pallas_call(
        functools.partial(kernel, n_cand, n_tp, cap),
        out_shape=jax.ShapeDtypeStruct((8, max(local, flat)), F32),
        in_specs=[vmem] * 7 + [hbm] * 3,
        out_specs=vmem,
        scratch_shapes=[
            pltpu.VMEM((2, n_tp, width + flat, chunk), BF16),
            pltpu.VMEM((2, n_tp, 1, chunk), F32),
            pltpu.VMEM((2, hidden, chunk), BF16),
            pltpu.VMEM((2, chunk, width), BF16),
            pltpu.VMEM((BATCH, hidden), BF16),
            pltpu.VMEM((n_work, BATCH, width), F32),
            pltpu.VMEM((n_work, n_tp, own, width), F32),
            pltpu.VMEM((n_work, BATCH, width), BF16),
            pltpu.VMEM((n_work, own, width), BF16),
            pltpu.VMEM((n_work, own, width), F32),
            pltpu.VMEM((n_work, own, width), F32),
            pltpu.VMEM((batches, rows, width), F32),
            pltpu.VMEM((rows, flat), BF16),
            pltpu.VMEM((n_mem, 2 * cap, flat), BF16),
            pltpu.VMEM((n_cand, rows, flat), F32),
            pltpu.VMEM((n_cand, 8, rows), F32),
            pltpu.VMEM((returned * batches, 1, rows), F32),
            dma((2,)), dma((2,)), dma((2,)),
            dma((2, n_tp)), dma((2, n_tp)),
            dma((2, n_tp)), dma((2, n_tp)),
            dma((2, 4, n_tp // 4 + 2)), dma((2, n_tp)),
            dma((n_mem,)), dma((n_mem,)),
            dma((n_cand,)), dma((n_cand,)),
            dma((n_cand,)), dma((n_cand,)),
            dma((n_work, n_own)), dma((n_work, n_tp)),
            dma((n_work, n_tp)), dma((n_work, n_own)),
            dma((total,)), dma((returned,)),
        ],
        compiler_params=pltpu.CompilerParams(has_side_effects=True, vmem_limit_bytes=56 << 20),
    )(
        start_state.reshape(1, -1), goal.reshape(1, -1), mean_prev.reshape(1, -1),
        std_prev.reshape(1, -1), noise, members.reshape(1, -1), elites.reshape(1, -1), w_in, w_hid, w_out,
    )
    scores, new_mean, new_std = pl.pallas_call(
        unpack,
        out_shape=(
            jax.ShapeDtypeStruct((1, local), F32),
            jax.ShapeDtypeStruct((1, flat), F32),
            jax.ShapeDtypeStruct((1, flat), F32),
        ),
        in_specs=[vmem],
        out_specs=(vmem,) * 3,
    )(packed)
    return scores.reshape(-1), new_mean.reshape(-1), new_std.reshape(-1)


def solution(mesh):
    placed = (
        P(), P(), P(), P(), P("cand", None), P("cand", None), P(),
        P(None, None, "tp"), P(None, None, "tp"), P(None, "tp", None),
    )
    return jax.shard_map(
        functools.partial(on_device, mesh.shape["cand"], mesh.shape["tp"]),
        mesh=mesh, in_specs=placed, out_specs=(P("cand"), P(), P()), check_vma=False,
    )
```

time: 116 us -> 93.2 us (0.80)
  Pallas kernels: 110 us -> 92.3 us
  local copies, waits for them, and re-layouts: 4.96 us -> 0 us
    pallas_call x1 -> x2, Pallas kernels: 110 us -> 92.3 us  [the longest x1 91.1 us: on_device(): pl.pallas_call(functools.partial(kernel, n_cand, n_tp, cap), out_shape=ja...]
    unnamed x4 -> x0, local copies, waits for them, and re-layouts: 4.96 us -> none
where the time goes in v1:
time: 93.2 us; the launch traced here: 93 us
  Pallas kernels  92.3 us (99%)
    pallas_call x1, Pallas kernels, on_device(): pl.pallas_call(functools.partial(kernel, n_cand, n_tp, cap), out_shape=ja...  91.1 us

profile of v1, /device:TPU:0, one launch (start us, length us, event | category | flops | bytes accessed | tf_op | source)
XLA Modules:
  0.0 93.0 jit_solution(9111604385416356213)
XLA Ops:
  0.6 91.1 %shard_map.121.packed_ref = f32[8,192]{1,0:T(8,128)} custom-call(f32[1,128]{1,0:T(1,128)} %bitcast.10, f32[1,128]{1,0:T(1,128)} %bitcast.11, f32[1,128]{1,0:T(1,128)} %bitcast.12, f32[1,128]{1,0:T(1,128)} %bitcast.13, f32[192,128]{1,0:T(8,128)} %noise_ref.1, s32[1,192]{1,0:T(1,128)} %bitcast.9, s32[1,96]{1,0:T(1,128)} %bitcast.14, ...), custom_call_target="tpu_custom_call" | custom-call | tf_op jit(solution)/shard_map/pallas_call | solution.py:451
  91.7 1.3 %shard_map.122 = (f32[1,192]{1,0:T(1,128)}, f32[1,128]{1,0:T(1,128)}, f32[1,128]{1,0:T(1,128)}) custom-call(f32[8,192]{1,0:T(8,128)} %shard_map.121.packed_ref), custom_call_target="tpu_custom_call" | custom-call | tf_op jit(solution)/shard_map/pallas_call | solution.py:490

commit v2 on v1

--- a/solution.py
+++ b/solution.py
@@ -72,7 +72,7 @@
 
     def wa_copy(mi, src, d, tt):
         return remote(
-            win_hbm.at[first + mi, pl.ds(width, a_dim), :], win_v.at[mi, src, pl.ds(width, a_dim), :],
+            win_v.at[mi, src, pl.ds(width, a_dim), :], win_v.at[mi, src, pl.ds(width, a_dim), :],
             wa_s.at[mi, d], wa_r.at[mi, src], c, tt)
 
     def bias_copy(mi, src, d, tt):
@@ -108,8 +108,6 @@
             win_hbm.at[first + mi, rows_s, :], win_v.at[mi, src, rows_s, :], ws_s.at[mi, 0, 0], ws_r.at[mi, src], c, t)
 
     def ws_serve():
-        for mi in range(2):
-            ws_own(mi, lambda cp: cp.start)
         for hop in range(1, n_z):
             for mi in range(2):
                 for up in (True, False):
@@ -135,13 +133,18 @@
     def wout_load(mi):
         return pltpu.make_async_copy(wout_hbm.at[first + mi], wout_v.at[mi], wout_sem.at[mi])
 
+    entered = pltpu.get_barrier_semaphore()
+    for kc in range(n_cand):
+        for kt in range(n_tp):
+            if kc + kt:
+                pl.semaphore_signal(
+                    entered, inc=1, device_id={"cand": lax.rem(c + kc, n_cand), "tp": tp_peer(kt)},
+                    device_id_type=pl.DeviceIdType.MESH)
+
     @pl.when(worker)
     def _():
         for mi in range(2):
             win_load(mi).start()
-        for mi in range(2):
-            for d in range(1, n_tp):
-                wa_copy(mi, t, d, tp_peer(d)).start()
         for mi in range(2):
             whid_load(mi).start()
             wout_load(mi).start()
@@ -165,9 +168,6 @@
             act_send.at[pl.ds(2 * i * cap, 2 * cap), :], act_rx.at[m], act_s.at[i], act_r.at[m],
             group + 2 * i + 1, t)
 
-    for i in range(n_mem // 2):
-        pl.when(c != group + 2 * i + 1)(act_copy(i).start)
-
     @pl.when(worker)
     def _():
         act_rx[m] = act_send[pl.ds(pl.multiple_of(first * cap, cap), 2 * cap), :]
@@ -176,10 +176,25 @@
             win_load(mi).wait()
             bias_v[mi, t] = jnp.dot(
                 half_start, win_v[mi, t, 0:width, :], preferred_element_type=F32)[0:1]
+
+    pl.semaphore_wait(entered, n_cand * n_tp - 1)
+    for i in range(n_mem // 2):
+        pl.when(c != group + 2 * i + 1)(act_copy(i).start)
+
+    @pl.when(worker)
+    def _():
+        for mi in range(2):
             for d in range(1, n_tp):
+                wa_copy(mi, t, d, tp_peer(d)).start()
                 bias_copy(mi, t, d, tp_peer(d)).start()
 
     lane = lax.broadcasted_iota(jnp.int32, (local, 128), 1)
+
+    @pl.when(jnp.logical_not(worker))
+    def _():
+        for mi in range(2):
+            ws_own(mi, lambda cp: cp.start)
+
     numbers = c * local + lax.broadcasted_iota(jnp.int32, (local, 1), 0)
     chosen = jnp.sum((numbers == elites_ref[...]).astype(F32), axis=1, keepdims=True)
     action_cost = jnp.sum(actions * actions, axis=1, keepdims=True) * (0.1 / a_dim)
@@ -482,7 +497,8 @@
             dma((n_work, n_tp)), dma((n_work, n_own)),
             dma((total,)), dma((returned,)),
         ],
-        compiler_params=pltpu.CompilerParams(has_side_effects=True, vmem_limit_bytes=56 << 20),
+        compiler_params=pltpu.CompilerParams(
+            collective_id=0, has_side_effects=True, vmem_limit_bytes=56 << 20),
     )(
         start_state.reshape(1, -1), goal.reshape(1, -1), mean_prev.reshape(1, -1),
         std_prev.reshape(1, -1), noise, members.reshape(1, -1), elites.reshape(1, -1), w_in, w_hid, w_out,

time: 93.2 us -> 90 us (0.966)
  Pallas kernels: 92.3 us -> 89.1 us
    pallas_call x1, Pallas kernels: 91.1 us -> 87.9 us  [on_device(): pl.pallas_call(functools.partial(kernel, n_cand, n_tp, cap), out_shape=ja...]
where the time goes in v2:
time: 90 us; the launch traced here: 89.8 us
  Pallas kernels  89.1 us (99%)
    pallas_call x1, Pallas kernels, on_device(): pl.pallas_call(functools.partial(kernel, n_cand, n_tp, cap), out_shape=ja...  87.9 us

profile of v2, /device:TPU:0, one launch (start us, length us, event | category | flops | bytes accessed | tf_op | source)
XLA Modules:
  0.0 89.8 jit_solution(10699782133739996937)
XLA Ops:
  0.6 87.9 %shard_map.121.packed_ref = f32[8,192]{1,0:T(8,128)} custom-call(f32[1,128]{1,0:T(1,128)} %bitcast.10, f32[1,128]{1,0:T(1,128)} %bitcast.11, f32[1,128]{1,0:T(1,128)} %bitcast.12, f32[1,128]{1,0:T(1,128)} %bitcast.13, f32[192,128]{1,0:T(8,128)} %noise_ref.1, s32[1,192]{1,0:T(1,128)} %bitcast.9, s32[1,96]{1,0:T(1,128)} %bitcast.14, ...), custom_call_target="tpu_custom_call" | custom-call | tf_op jit(solution)/shard_map/pallas_call | solution.py:466
  88.5 1.3 %shard_map.122 = (f32[1,192]{1,0:T(1,128)}, f32[1,128]{1,0:T(1,128)}, f32[1,128]{1,0:T(1,128)}) custom-call(f32[8,192]{1,0:T(8,128)} %shard_map.121.packed_ref), custom_call_target="tpu_custom_call" | custom-call | tf_op jit(solution)/shard_map/pallas_call | solution.py:506

commit v3 on v2

--- a/solution.py
+++ b/solution.py
@@ -81,47 +81,51 @@
     n_z = 4
     n_y = n_tp // n_z
     z, y = t // n_y, lax.rem(t, n_y)
-    rows_s = pl.ds(0, width)
-
-    def ws_copy(mi, src_z, e, own_slice, cc, tt):
+    pieces = 2
+    piece = width // pieces
+
+    def rows_s(u):
+        return pl.ds(pl.multiple_of(lax.rem(u, pieces) * piece, piece), piece)
+
+    def ws_copy(u, src_z, e, own_slice, cc, tt):
         src = src_z * n_y + y
-        held = win_hbm.at[first + mi, rows_s, :] if own_slice else win_v.at[mi, src, rows_s, :]
-        return remote(held, win_v.at[mi, src, rows_s, :], ws_s.at[mi, src_z, e], ws_r.at[mi, src], cc, tt)
-
-    def ws_own(mi, act):
-        pl.when(z < n_z - 1)(act(ws_copy(mi, z, n_y, True, c, t + n_y)))
-        pl.when(z > 0)(act(ws_copy(mi, z, n_y + 1, True, c, t - n_y)))
+        held = win_hbm.at[first + u // pieces, rows_s(u), :] if own_slice else win_v.at[u // pieces, src, rows_s(u), :]
+        return remote(held, win_v.at[u // pieces, src, rows_s(u), :], ws_s.at[u, src_z, e], ws_r.at[u, src], cc, tt)
+
+    def ws_own(u, act):
+        pl.when(z < n_z - 1)(act(ws_copy(u, z, n_y, True, c, t + n_y)))
+        pl.when(z > 0)(act(ws_copy(u, z, n_y + 1, True, c, t - n_y)))
         for e in range(n_y):
-            pl.when(y != e)(act(ws_copy(mi, z, e, True, c + 1, z * n_y + e)))
-
-    def ws_relayed(mi, hop, up, act):
+            pl.when(y != e)(act(ws_copy(u, z, e, True, c + 1, z * n_y + e)))
+
+    def ws_relayed(u, hop, up, act):
         src_z = z - hop if up else z + hop
         there = src_z >= 0 if up else src_z < n_z
         onward = z < n_z - 1 if up else z > 0
-        beyond = ws_copy(mi, src_z, n_y if up else n_y + 1, False, c, t + n_y if up else t - n_y)
+        beyond = ws_copy(u, src_z, n_y if up else n_y + 1, False, c, t + n_y if up else t - n_y)
         pl.when(jnp.logical_and(there, onward))(act(beyond))
         for e in range(n_y):
-            pl.when(there)(act(ws_copy(mi, src_z, e, False, c + 1, z * n_y + e)))
-
-    def ws_arrived(mi, src):
+            pl.when(there)(act(ws_copy(u, src_z, e, False, c + 1, z * n_y + e)))
+
+    def ws_arrived(u, src):
         return remote(
-            win_hbm.at[first + mi, rows_s, :], win_v.at[mi, src, rows_s, :], ws_s.at[mi, 0, 0], ws_r.at[mi, src], c, t)
+            win_hbm.at[first + u // pieces, rows_s(u), :], win_v.at[u // pieces, src, rows_s(u), :], ws_s.at[u, 0, 0], ws_r.at[u, src], c, t)
 
     def ws_serve():
         for hop in range(1, n_z):
-            for mi in range(2):
+            for u in range(2 * pieces):
                 for up in (True, False):
                     src_z = z - hop if up else z + hop
                     there = src_z >= 0 if up else src_z < n_z
-                    pl.when(there)(ws_arrived(mi, src_z * n_y + y).wait_recv)
-                    ws_relayed(mi, hop, up, lambda cp: cp.start)
+                    pl.when(there)(ws_arrived(u, src_z * n_y + y).wait_recv)
+                    ws_relayed(u, hop, up, lambda cp: cp.start)
 
     def ws_served():
-        for mi in range(2):
-            ws_own(mi, lambda cp: cp.wait_send)
+        for u in range(2 * pieces):
+            ws_own(u, lambda cp: cp.wait_send)
             for hop in range(1, n_z):
                 for up in (True, False):
-                    ws_relayed(mi, hop, up, lambda cp: cp.wait_send)
+                    ws_relayed(u, hop, up, lambda cp: cp.wait_send)
 
     def win_load(mi):
         return pltpu.make_async_copy(
@@ -192,8 +196,8 @@
 
     @pl.when(jnp.logical_not(worker))
     def _():
-        for mi in range(2):
-            ws_own(mi, lambda cp: cp.start)
+        for u in range(2 * pieces):
+            ws_own(u, lambda cp: cp.start)
 
     numbers = c * local + lax.broadcasted_iota(jnp.int32, (local, 1), 0)
     chosen = jnp.sum((numbers == elites_ref[...]).astype(F32), axis=1, keepdims=True)
@@ -305,7 +309,8 @@
             @pl.when(jnp.logical_and(step == 1, q == 0))
             def _():
                 for d in range(1, n_tp):
-                    ws_arrived(mi, tp_from(d)).wait_recv()
+                    for h in range(pieces):
+                        ws_arrived(mi * pieces + h, tp_from(d)).wait_recv()
 
             for i in range(n_own):
                 pl.when(t != owners[i])(ag_copy(k, i, t).wait_recv)
@@ -339,7 +344,7 @@
 
                 @pl.when(owner)
                 def _():
-                    lax.fori_loop(k * (k - 1) // 2, jnp.minimum(k * (k + 1) // 2, n_work), turn, 0)
+                    lax.fori_loop((k + 1) // 2, 1 + k * (k - 1) // 2, turn, 0)
 
                 return carry
 
@@ -489,7 +494,7 @@
             dma((2,)), dma((2,)), dma((2,)),
             dma((2, n_tp)), dma((2, n_tp)),
             dma((2, n_tp)), dma((2, n_tp)),
-            dma((2, 4, n_tp // 4 + 2)), dma((2, n_tp)),
+            dma((4, 4, n_tp // 4 + 2)), dma((4, n_tp)),
             dma((n_mem,)), dma((n_mem,)),
             dma((n_cand,)), dma((n_cand,)),
             dma((n_cand,)), dma((n_cand,)),

time: 90 us -> 87.7 us (0.974)
  Pallas kernels: 89.1 us -> 86.9 us
    pallas_call x1, Pallas kernels: 87.9 us -> 85.6 us  [on_device(): pl.pallas_call(functools.partial(kernel, n_cand, n_tp, cap), out_shape=ja...]
where the time goes in v3:
time: 87.7 us; the launch traced here: 87.5 us
  Pallas kernels  86.9 us (99%)
    pallas_call x1, Pallas kernels, on_device(): pl.pallas_call(functools.partial(kernel, n_cand, n_tp, cap), out_shape=ja...  85.6 us

profile of v3, /device:TPU:0, one launch (start us, length us, event | category | flops | bytes accessed | tf_op | source)
XLA Modules:
  0.0 87.5 jit_solution(7196962508840938372)
XLA Ops:
  0.6 85.6 %shard_map.121.packed_ref = f32[8,192]{1,0:T(8,128)} custom-call(f32[1,128]{1,0:T(1,128)} %bitcast.10, f32[1,128]{1,0:T(1,128)} %bitcast.11, f32[1,128]{1,0:T(1,128)} %bitcast.12, f32[1,128]{1,0:T(1,128)} %bitcast.13, f32[192,128]{1,0:T(8,128)} %noise_ref.1, s32[1,192]{1,0:T(1,128)} %bitcast.9, s32[1,96]{1,0:T(1,128)} %bitcast.14, ...), custom_call_target="tpu_custom_call" | custom-call | tf_op jit(solution)/shard_map/pallas_call | solution.py:471
  86.2 1.3 %shard_map.122 = (f32[1,192]{1,0:T(1,128)}, f32[1,128]{1,0:T(1,128)}, f32[1,128]{1,0:T(1,128)}) custom-call(f32[8,192]{1,0:T(8,128)} %shard_map.121.packed_ref), custom_call_target="tpu_custom_call" | custom-call | tf_op jit(solution)/shard_map/pallas_call | solution.py:511
